TPU v7x, 128 devices: a whole 4x4x4 slice. The times are simulated.
128 devices in a mesh: member: 8 (over z, core), region: 16 (over y, x).
Axes of the slice: x: 4, y: 4, z: 4, core: 2. Of those that a mesh axis runs over, the one named last changes fastest.
Arguments:
- ensemble: bfloat16 [256, 1024, 512], P(('member', 'region')), may hold values from -6 to 6
- obs_site: int32 [1024, 2048], P(('member', 'region')), may hold values from 0 to 511
- obs_blocks: int32 [1024], P(('member', 'region')), may hold values from 1 to 16
- obs_precision: bfloat16 [1024, 2048], P(('member', 'region')), may hold values from 0.049804688 to 1
- obs_innovation: bfloat16 [1024, 2048], P(('member', 'region')), may hold values from -6 to 6
Outputs:
- analysis: bfloat16 [256, 1024, 512], P(('member', 'region'))
Inputs may be any that keep to these rules, and one draw needn't show every extreme that they name: Only the first obs_blocks[p] blocks of 128 observations of patch p are used.
All inputs are finite; a program needn't handle non-finite values.
Results may differ from a plain program's by a relative error of at most 0.0062.
Values may be sent and summed in bfloat16 or wider, within the bound.
A program may use at most 64 MiB of HBM per device.

v0:
```python
import functools

import jax
import jax.numpy as jnp
from jax import lax
from jax.experimental import pallas as pl
from jax.experimental.pallas import tpu as pltpu
from jax.sharding import PartitionSpec as P

K = 256
S = 512
SLOTS = 2048
OB = 128
ITERS = 6
DEVICES = 128
PATCHES = 8
GROUPS = 2
QUAD = PATCHES // GROUPS
STRIDE = 37
MESH = pl.DeviceIdType.MESH
F32 = jnp.float32
BF16 = jnp.bfloat16


def dot(left, right):
    return jnp.dot(left, right, preferred_element_type=F32)


def dot_t(left, right):
    return lax.dot_general(left, right, (((1,), (1,)), ((), ())), preferred_element_type=F32)


def split(value):
    high = value.astype(BF16)
    return high, (value - high.astype(F32)).astype(BF16)


def iota(shape, axis):
    return lax.broadcasted_iota(jnp.int32, shape, axis)


def peer(member, region, offset):
    x = lax.rem(lax.rem(region, 4) + lax.rem(offset, 4), 4)
    y = lax.rem(lax.div(region, 4) + lax.rem(lax.div(offset, 4), 4), 4)
    z = lax.rem(lax.div(member, 2) + lax.rem(lax.div(offset, 16), 4), 4)
    core = lax.rem(lax.rem(member, 2) + lax.div(offset, 64), 2)
    return z * 2 + core, y * 4 + x


def enter(member, region):
    barrier = pltpu.get_barrier_semaphore()
    members = [lax.rem(member + step, 8) for step in range(8)]
    regions = [lax.rem(region + step, 16) for step in range(16)]
    for outer in range(8):
        for inner in range(16):
            if outer or inner:
                pl.semaphore_signal(
                    barrier,
                    inc=1,
                    device_id=(members[outer], regions[inner]),
                    device_id_type=MESH,
                )
    pl.semaphore_wait(barrier, DEVICES - 1)


def histogram(site_ref, blocks_ref, weight32, value32, weights, sides):
    lanes = iota((1, SLOTS), 1)
    rows = iota((16, SLOTS), 0)
    quarter = lax.rem(rows, 4)

    def one(patch, carry):
        site = site_ref[pl.ds(patch, 1), :]
        live = lanes < blocks_ref[patch] * OB
        weight = jnp.where(live, weight32[pl.ds(patch, 1), :], 0.0)
        product = weight * value32[pl.ds(patch, 1), :]
        high = product.astype(BF16).astype(F32)
        low = product - high
        picked = jnp.where(rows < 4, weight, jnp.where(rows < 8, high, low))
        upper = jnp.where(quarter == lax.shift_right_logical(site, 7), picked, 0.0).astype(BF16)
        lower = jnp.where(iota((128, SLOTS), 0) == jnp.bitwise_and(site, 127), 1.0, 0.0).astype(BF16)
        sums = dot_t(upper, lower)
        weights[patch] = sums[0:4]
        sides[patch] = sums[4:8] + sums[8:12]
        return carry

    lax.fori_loop(0, PATCHES, one, 0)


def as_row(table):
    return jnp.concatenate([table[part : part + 1, :] for part in range(4)], axis=1)


def analyse(group, inbox, outbox, place_in, place_out, weights, sides, state, pert, work, zed, why, mean):
    landed = inbox.reshape(GROUPS, 4, 4 * K, 128)
    leaving = outbox.reshape(GROUPS, 4, 4 * K, 128)
    quads = range(QUAD)

    for block in range(4):
        rows = slice(256 * block, 256 * block + 256)
        for half in range(2):
            tile = jnp.concatenate([landed[group, 2 * half, rows, :], landed[group, 2 * half + 1, rows, :]], axis=1)
            placed = dot(place_in[...], tile).astype(BF16)
            for quad in quads:
                state[quad, 64 * block : 64 * block + 64, 256 * half : 256 * half + 256] = placed[
                    64 * quad : 64 * quad + 64
                ]

    eye = jnp.where(iota((K, K), 0) == iota((K, K), 1), 1.0, 0.0).astype(F32)
    scales, rights = [], []
    for quad in quads:
        values = state[quad].astype(F32)
        centre = jnp.sum(values, axis=0, keepdims=True) * (1.0 / K)
        mean[quad] = centre
        around = (values - centre).astype(BF16)
        pert[quad] = around
        work[quad, 0:K, :] = (around.astype(F32) * as_row(weights[group * QUAD + quad])).astype(BF16)
        side = as_row(sides[group * QUAD + quad])
        high = side.astype(BF16).astype(F32)
        work[quad, K : K + 16, :] = jnp.where(
            iota((16, S), 0) == 0, high, jnp.where(iota((16, S), 0) == 1, side - high, 0.0)
        ).astype(BF16)
    for quad in quads:
        sums = dot_t(work[quad], pert[quad])
        right = sums[K : K + 1] + sums[K + 1 : K + 2]
        amat = sums[0:K] + 255.0 * eye
        square = jnp.sum(jnp.sum(amat * amat, axis=0, keepdims=True), axis=1, keepdims=True)
        scale = jnp.sqrt(square)
        scales.append(scale)
        rights.append(right)
        why[quad] = amat / scale

    for quad in quads:
        first = why[quad]
        high = first.astype(BF16)
        zed[quad] = 1.5 * eye - 0.5 * first
        why[quad] = 1.5 * first - 0.5 * dot(high, high)
    for step in range(1, ITERS):
        exact = step >= ITERS - 2
        last = step == ITERS - 1
        for quad in quads:
            z, y = zed[quad], why[quad]
            if exact:
                z_high, z_low = split(z)
                y_high, y_low = split(y)
                w = dot(z_high, y_high) + dot(z_high, y_low) + dot(z_low, y_high)
                w_high, w_low = split(w)
                zed[quad] = 1.5 * z - 0.5 * (dot(z_high, w_high) + dot(z_high, w_low) + dot(z_low, w_high))
                if not last:
                    why[quad] = 1.5 * y - 0.5 * (dot(y_high, w_high) + dot(y_high, w_low) + dot(y_low, w_high))
            else:
                z_high, y_high = z.astype(BF16), y.astype(BF16)
                w_high = dot(z_high, y_high).astype(BF16)
                zed[quad] = 1.5 * z - 0.5 * dot(z_high, w_high)
                why[quad] = 1.5 * y - 0.5 * dot(y_high, w_high)

    for quad in quads:
        z = zed[quad]
        once = jnp.sum(z * rights[quad], axis=1, keepdims=True)
        twice = jnp.sum(z * once, axis=0, keepdims=True)
        factor = jnp.sqrt(255.0 / scales[quad])
        coef = (twice / scales[quad] + factor * z).astype(BF16)
        state[quad] = (mean[quad] + dot(coef, pert[quad])).astype(BF16)

    for block in range(4):
        rows = slice(256 * block, 256 * block + 256)
        for half in range(2):
            tile = jnp.concatenate(
                [state[quad, 64 * block : 64 * block + 64, 256 * half : 256 * half + 256] for quad in quads], axis=0
            )
            placed = dot(place_out[...], tile).astype(BF16)
            leaving[group, 2 * half, rows, :] = placed[:, 0:128]
            leaving[group, 2 * half + 1, rows, :] = placed[:, 128:256]


def kernel(
    ens_ref, site_ref, blocks_ref, precision_ref, innovation_ref, out_ref,
    inbox, outbox, place_in, place_out, weight32, value32, weights, sides, state, pert, work, zed, why, mean,
    in_send, in_recv, in_own, out_send, out_recv, out_own,
):
    member, region = lax.axis_index("member"), lax.axis_index("region")
    me = member * 16 + region

    enter(member, region)

    for group in range(GROUPS):
        pairs = pl.ds(2 * group, 2)

        def send(index, carry):
            to_member, to_region = peer(member, region, lax.rem(index * STRIDE, DEVICES))
            to = to_member * 16 + to_region
            for row in range(2):
                pltpu.make_async_remote_copy(
                    src_ref=ens_ref.at[row, to, :, pairs],
                    dst_ref=inbox.at[group, :, me, row],
                    send_sem=in_send.at[group],
                    recv_sem=in_recv.at[group],
                    device_id=(to_member, to_region),
                    device_id_type=MESH,
                ).start()
            return carry

        lax.fori_loop(1, DEVICES, send, 0)
        for row in range(2):
            pltpu.make_async_copy(
                ens_ref.at[row, me, :, pairs], inbox.at[group, :, me, row], in_own.at[group, row]
            ).start()

    out_row, in_row = iota((256, 256), 0), iota((256, 256), 1)
    moved = jnp.bitwise_and(out_row, 63) * 4 + lax.shift_right_logical(out_row, 6)
    place_in[...] = jnp.where(in_row == moved, 1.0, 0.0).astype(BF16)
    moved = jnp.bitwise_and(out_row, 3) * 64 + lax.shift_right_logical(out_row, 2)
    place_out[...] = jnp.where(in_row == moved, 1.0, 0.0).astype(BF16)
    weight32[...] = precision_ref[...].astype(F32)
    value32[...] = innovation_ref[...].astype(F32)
    histogram(site_ref, blocks_ref, weight32, value32, weights, sides)

    def one_group(group, carry):
        pairs = pl.ds(2 * group, 2)
        for row in range(2):
            pltpu.make_async_copy(
                ens_ref.at[row, me, :, pairs], inbox.at[group, :, me, row], in_own.at[group, row]
            ).wait()
        arrived = inbox.at[group, :, pl.ds(0, DEVICES - 1)]
        pltpu.make_async_copy(arrived, arrived, in_recv.at[group]).wait()

        analyse(
            group, inbox, outbox, place_in, place_out, weights, sides, state, pert, work, zed, why, mean
        )

        def send(index, carry):
            to_member, to_region = peer(member, region, lax.rem(index * STRIDE, DEVICES))
            to = to_member * 16 + to_region
            for row in range(2):
                pltpu.make_async_remote_copy(
                    src_ref=outbox.at[group, :, to, row],
                    dst_ref=out_ref.at[row, me, :, pairs],
                    send_sem=out_send,
                    recv_sem=out_recv,
                    device_id=(to_member, to_region),
                    device_id_type=MESH,
                ).start()
            return carry

        lax.fori_loop(1, DEVICES, send, 0)
        for row in range(2):
            pltpu.make_async_copy(
                outbox.at[group, :, me, row], out_ref.at[row, me, :, pairs], out_own.at[group, row]
            ).start()
        return carry

    lax.fori_loop(0, GROUPS, one_group, 0)

    for group in range(GROUPS):
        sent = inbox.at[group, :, pl.ds(0, DEVICES - 1)]
        pltpu.make_async_copy(sent, sent, in_send.at[group]).wait()
        for row in range(2):
            pltpu.make_async_copy(
                outbox.at[group, :, me, row], out_ref.at[row, me, :, pl.ds(2 * group, 2)], out_own.at[group, row]
            ).wait()
    sent = outbox.at[:, :, pl.ds(0, DEVICES - 1)]
    pltpu.make_async_copy(sent, sent, out_send).wait()
    arrived = out_ref.at[:, pl.ds(0, DEVICES - 1)]
    pltpu.make_async_copy(arrived, arrived, out_recv).wait()


def local(ensemble, obs_site, obs_blocks, obs_precision, obs_innovation):
    pairs = ensemble.reshape(2, DEVICES, PATCHES, 4, 128).transpose(0, 1, 3, 2, 4)
    pairs = pairs.reshape(2, DEVICES, 4, 4, 2, 128)
    vmem = pl.BlockSpec(memory_space=pltpu.VMEM)
    hbm = pl.BlockSpec(memory_space=pltpu.HBM)
    result = pl.pallas_call(
        kernel,
        out_shape=jax.ShapeDtypeStruct(pairs.shape, BF16),
        in_specs=[hbm, vmem, pl.BlockSpec(memory_space=pltpu.SMEM), vmem, vmem],
        out_specs=hbm,
        scratch_shapes=[
            pltpu.VMEM((GROUPS, 4, DEVICES, 2, 2, 2, 128), BF16),
            pltpu.VMEM((GROUPS, 4, DEVICES, 2, 2, 2, 128), BF16),
            pltpu.VMEM((256, 256), BF16),
            pltpu.VMEM((256, 256), BF16),
            pltpu.VMEM((PATCHES, SLOTS), F32),
            pltpu.VMEM((PATCHES, SLOTS), F32),
            pltpu.VMEM((PATCHES, 4, 128), F32),
            pltpu.VMEM((PATCHES, 4, 128), F32),
            pltpu.VMEM((QUAD, K, S), BF16),
            pltpu.VMEM((QUAD, K, S), BF16),
            pltpu.VMEM((QUAD, K + 16, S), BF16),
            pltpu.VMEM((QUAD, K, K), F32),
            pltpu.VMEM((QUAD, K, K), F32),
            pltpu.VMEM((QUAD, 1, S), F32),
            pltpu.SemaphoreType.DMA((GROUPS,)),
            pltpu.SemaphoreType.DMA((GROUPS,)),
            pltpu.SemaphoreType.DMA((GROUPS, 2)),
            pltpu.SemaphoreType.DMA,
            pltpu.SemaphoreType.DMA,
            pltpu.SemaphoreType.DMA((GROUPS, 2)),
        ],
        compiler_params=pltpu.CompilerParams(
            collective_id=0, has_side_effects=True, vmem_limit_bytes=56 * 1024 * 1024
        ),
    )(pairs, obs_site, obs_blocks, obs_precision, obs_innovation)
    result = result.reshape(2, DEVICES, 4, PATCHES, 128).transpose(0, 1, 3, 2, 4)
    return result.reshape(2, DEVICES * PATCHES, S)


def solution(mesh):
    axes = ("member", "region")
    rows = P(axes, None)
    return jax.shard_map(
        local,
        mesh=mesh,
        in_specs=(P(axes, None, None), rows, P(axes), rows, rows),
        out_specs=P(axes, None, None),
        check_vma=False,
    )
```

profile of v0, /device:TPU:1, one launch (start us, length us, event | category | flops | bytes accessed | tf_op | source)
XLA Modules:
  0.0 70.9 jit_solution(7317973369305398656)
XLA Ops:
  0.0 67.9 %shard_map.55 = bf16[2,128,4,4,2,128]{5,4,3,2,1,0:T(2,128)(2,1)} custom-call(bf16[2,128,4,4,2,128]{5,4,3,2,1,0:T(2,128)(2,1)} %bitcast.11, s32[8,2048]{1,0:T(8,128)} %site_ref.1, s32[8]{0:T(128)} %blocks_ref.1, bf16[8,2048]{1,0:T(8,128)(2,1)} %precision_ref.1, bf16[8,2048]{1,0:T(8,128)(2,1)} %innovation_ref.1), custom_call_target="tpu_custom_call" | custom-call | tf_op jit(solution)/shard_map/pallas_call | solution.py:271
  67.9 3.0 %copy.7 = bf16[2,1024,512]{2,1,0:T(8,128)(2,1)} copy(bf16[2,1024,512]{2,1,0:T(8,128)(2,1)} %bitcast.10) | data formatting | bytes 4194304
where the time goes:
time: 71.1 us; the launch traced here: 70.9 us
  Pallas kernels  67.9 us (95%)
  local copies, waits for them, and re-layouts  3.05 us (4%)
    pallas_call x1, Pallas kernels, local(): pl.pallas_call(kernel, out_shape=jax.ShapeDtypeStruct(pairs.shape, BF16),...  67.9 us
    unnamed x1, local copies, waits for them, and re-layouts  3.05 us

commit v1 on v0

--- a/solution.py
+++ b/solution.py
@@ -12,6 +12,7 @@
 SLOTS = 2048
 OB = 128
 ITERS = 6
+EXACT_FROM = 4
 DEVICES = 128
 PATCHES = 8
 GROUPS = 2
@@ -90,7 +91,7 @@
     return jnp.concatenate([table[part : part + 1, :] for part in range(4)], axis=1)
 
 
-def analyse(group, inbox, outbox, place_in, place_out, weights, sides, state, pert, work, zed, why, mean):
+def analyse(group, inbox, outbox, place_in, place_out, weights, sides, state, pert, work, iterate, high_part, low_part, product, product_low, coef, mean):
     landed = inbox.reshape(GROUPS, 4, 4 * K, 128)
     leaving = outbox.reshape(GROUPS, 4, 4 * K, 128)
     quads = range(QUAD)
@@ -127,39 +128,53 @@
         scale = jnp.sqrt(square)
         scales.append(scale)
         rights.append(right)
-        why[quad] = amat / scale
-
-    for quad in quads:
-        first = why[quad]
-        high = first.astype(BF16)
-        zed[quad] = 1.5 * eye - 0.5 * first
-        why[quad] = 1.5 * first - 0.5 * dot(high, high)
+        first = amat / scale
+        iterate[quad, K:] = first
+        high_part[quad, K:] = first.astype(BF16)
+    for quad in quads:
+        first = iterate[quad, K:]
+        second = (eye - first * (1.0 / 3.0), first - dot(high_part[quad, K:], high_part[quad, K:]) * (1.0 / 3.0))
+        for part in range(2):
+            iterate[quad, K * part : K * part + K] = second[part]
+            high_part[quad, K * part : K * part + K] = second[part].astype(BF16)
+
     for step in range(1, ITERS):
-        exact = step >= ITERS - 2
+        exact = step >= EXACT_FROM
         last = step == ITERS - 1
+        third = 1.5 ** (2 * step) / 3.0
         for quad in quads:
-            z, y = zed[quad], why[quad]
+            z_high, y_high = high_part[quad, 0:K], high_part[quad, K:]
+            both = dot(z_high, y_high)
             if exact:
-                z_high, z_low = split(z)
-                y_high, y_low = split(y)
-                w = dot(z_high, y_high) + dot(z_high, y_low) + dot(z_low, y_high)
-                w_high, w_low = split(w)
-                zed[quad] = 1.5 * z - 0.5 * (dot(z_high, w_high) + dot(z_high, w_low) + dot(z_low, w_high))
+                both += dot(z_high, low_part[quad, K:]) + dot(low_part[quad, 0:K], y_high)
+                both = both * third
+                product_low[quad] = (both - both.astype(BF16).astype(F32)).astype(BF16)
+                product[quad] = both.astype(BF16)
+            else:
+                product[quad] = (both * third).astype(BF16)
+        for quad in quads:
+            for part in range(1 if last else 2):
+                rows = slice(K * part, K * part + K)
+                high = high_part[quad, rows]
+                moved = dot(high, product[quad])
+                if exact:
+                    moved += dot(high, product_low[quad]) + dot(low_part[quad, rows], product[quad])
+                after = iterate[quad, rows] - moved
+                iterate[quad, rows] = after
                 if not last:
-                    why[quad] = 1.5 * y - 0.5 * (dot(y_high, w_high) + dot(y_high, w_low) + dot(y_low, w_high))
-            else:
-                z_high, y_high = z.astype(BF16), y.astype(BF16)
-                w_high = dot(z_high, y_high).astype(BF16)
-                zed[quad] = 1.5 * z - 0.5 * dot(z_high, w_high)
-                why[quad] = 1.5 * y - 0.5 * dot(y_high, w_high)
-
-    for quad in quads:
-        z = zed[quad]
+                    high_part[quad, rows] = after.astype(BF16)
+                    if step + 1 >= EXACT_FROM:
+                        low_part[quad, rows] = (after - after.astype(BF16).astype(F32)).astype(BF16)
+
+    grown = 1.5**ITERS
+    for quad in quads:
+        z = iterate[quad, 0:K]
         once = jnp.sum(z * rights[quad], axis=1, keepdims=True)
         twice = jnp.sum(z * once, axis=0, keepdims=True)
-        factor = jnp.sqrt(255.0 / scales[quad])
-        coef = (twice / scales[quad] + factor * z).astype(BF16)
-        state[quad] = (mean[quad] + dot(coef, pert[quad])).astype(BF16)
+        factor = grown * jnp.sqrt(255.0 / scales[quad])
+        coef[quad] = (twice * (grown * grown / scales[quad]) + factor * z).astype(BF16)
+    for quad in quads:
+        state[quad] = (mean[quad] + dot(coef[quad], pert[quad])).astype(BF16)
 
     for block in range(4):
         rows = slice(256 * block, 256 * block + 256)
@@ -173,24 +188,30 @@
 
 
 def kernel(
-    ens_ref, site_ref, blocks_ref, precision_ref, innovation_ref, out_ref,
-    inbox, outbox, place_in, place_out, weight32, value32, weights, sides, state, pert, work, zed, why, mean,
-    in_send, in_recv, in_own, out_send, out_recv, out_own,
+    ens_ref, site_hbm, blocks_hbm, precision_hbm, innovation_hbm, out_ref,
+    site_ref, blocks_ref, precision_ref, innovation_ref, inbox, outbox, place_in, place_out, weight32, value32, weights, sides, state, pert, work, iterate, high_part, low_part, product, product_low, coef, mean,
+    obs_sem, in_send, in_recv, in_own, out_send, out_recv, out_own,
 ):
     member, region = lax.axis_index("member"), lax.axis_index("region")
     me = member * 16 + region
 
+    moves = (
+        pltpu.make_async_copy(site_hbm, site_ref, obs_sem.at[0]),
+        pltpu.make_async_copy(precision_hbm, precision_ref, obs_sem.at[1]),
+        pltpu.make_async_copy(innovation_hbm, innovation_ref, obs_sem.at[2]),
+        pltpu.make_async_copy(blocks_hbm, blocks_ref, obs_sem.at[3]),
+    )
+    for move in moves:
+        move.start()
     enter(member, region)
 
     for group in range(GROUPS):
-        pairs = pl.ds(2 * group, 2)
-
         def send(index, carry):
             to_member, to_region = peer(member, region, lax.rem(index * STRIDE, DEVICES))
             to = to_member * 16 + to_region
             for row in range(2):
                 pltpu.make_async_remote_copy(
-                    src_ref=ens_ref.at[row, to, :, pairs],
+                    src_ref=ens_ref.at[row, to, :, group],
                     dst_ref=inbox.at[group, :, me, row],
                     send_sem=in_send.at[group],
                     recv_sem=in_recv.at[group],
@@ -202,7 +223,7 @@
         lax.fori_loop(1, DEVICES, send, 0)
         for row in range(2):
             pltpu.make_async_copy(
-                ens_ref.at[row, me, :, pairs], inbox.at[group, :, me, row], in_own.at[group, row]
+                ens_ref.at[row, me, :, group], inbox.at[group, :, me, row], in_own.at[group, row]
             ).start()
 
     out_row, in_row = iota((256, 256), 0), iota((256, 256), 1)
@@ -210,21 +231,22 @@
     place_in[...] = jnp.where(in_row == moved, 1.0, 0.0).astype(BF16)
     moved = jnp.bitwise_and(out_row, 3) * 64 + lax.shift_right_logical(out_row, 2)
     place_out[...] = jnp.where(in_row == moved, 1.0, 0.0).astype(BF16)
+    for move in moves:
+        move.wait()
     weight32[...] = precision_ref[...].astype(F32)
     value32[...] = innovation_ref[...].astype(F32)
     histogram(site_ref, blocks_ref, weight32, value32, weights, sides)
 
     def one_group(group, carry):
-        pairs = pl.ds(2 * group, 2)
         for row in range(2):
             pltpu.make_async_copy(
-                ens_ref.at[row, me, :, pairs], inbox.at[group, :, me, row], in_own.at[group, row]
+                ens_ref.at[row, me, :, group], inbox.at[group, :, me, row], in_own.at[group, row]
             ).wait()
         arrived = inbox.at[group, :, pl.ds(0, DEVICES - 1)]
         pltpu.make_async_copy(arrived, arrived, in_recv.at[group]).wait()
 
         analyse(
-            group, inbox, outbox, place_in, place_out, weights, sides, state, pert, work, zed, why, mean
+            group, inbox, outbox, place_in, place_out, weights, sides, state, pert, work, iterate, high_part, low_part, product, product_low, coef, mean
         )
 
         def send(index, carry):
@@ -233,7 +255,7 @@
             for row in range(2):
                 pltpu.make_async_remote_copy(
                     src_ref=outbox.at[group, :, to, row],
-                    dst_ref=out_ref.at[row, me, :, pairs],
+                    dst_ref=out_ref.at[row, me, :, group],
                     send_sem=out_send,
                     recv_sem=out_recv,
                     device_id=(to_member, to_region),
@@ -244,7 +266,7 @@
         lax.fori_loop(1, DEVICES, send, 0)
         for row in range(2):
             pltpu.make_async_copy(
-                outbox.at[group, :, me, row], out_ref.at[row, me, :, pairs], out_own.at[group, row]
+                outbox.at[group, :, me, row], out_ref.at[row, me, :, group], out_own.at[group, row]
             ).start()
         return carry
 
@@ -255,7 +277,7 @@
         pltpu.make_async_copy(sent, sent, in_send.at[group]).wait()
         for row in range(2):
             pltpu.make_async_copy(
-                outbox.at[group, :, me, row], out_ref.at[row, me, :, pl.ds(2 * group, 2)], out_own.at[group, row]
+                outbox.at[group, :, me, row], out_ref.at[row, me, :, group], out_own.at[group, row]
             ).wait()
     sent = outbox.at[:, :, pl.ds(0, DEVICES - 1)]
     pltpu.make_async_copy(sent, sent, out_send).wait()
@@ -265,17 +287,20 @@
 
 def local(ensemble, obs_site, obs_blocks, obs_precision, obs_innovation):
     pairs = ensemble.reshape(2, DEVICES, PATCHES, 4, 128).transpose(0, 1, 3, 2, 4)
-    pairs = pairs.reshape(2, DEVICES, 4, 4, 2, 128)
-    vmem = pl.BlockSpec(memory_space=pltpu.VMEM)
+    pairs = pairs.reshape(2, DEVICES, 4, GROUPS, QUAD, 128)
     hbm = pl.BlockSpec(memory_space=pltpu.HBM)
     result = pl.pallas_call(
         kernel,
         out_shape=jax.ShapeDtypeStruct(pairs.shape, BF16),
-        in_specs=[hbm, vmem, pl.BlockSpec(memory_space=pltpu.SMEM), vmem, vmem],
-        out_specs=hbm,
+        in_specs=[hbm] * 5,
+        out_specs=pl.BlockSpec(memory_space=pl.ANY),
         scratch_shapes=[
-            pltpu.VMEM((GROUPS, 4, DEVICES, 2, 2, 2, 128), BF16),
-            pltpu.VMEM((GROUPS, 4, DEVICES, 2, 2, 2, 128), BF16),
+            pltpu.VMEM((PATCHES, SLOTS), jnp.int32),
+            pltpu.SMEM((PATCHES,), jnp.int32),
+            pltpu.VMEM((PATCHES, SLOTS), BF16),
+            pltpu.VMEM((PATCHES, SLOTS), BF16),
+            pltpu.VMEM((GROUPS, 4, DEVICES, 2, QUAD, 128), BF16),
+            pltpu.VMEM((GROUPS, 4, DEVICES, 2, QUAD, 128), BF16),
             pltpu.VMEM((256, 256), BF16),
             pltpu.VMEM((256, 256), BF16),
             pltpu.VMEM((PATCHES, SLOTS), F32),
@@ -285,9 +310,14 @@
             pltpu.VMEM((QUAD, K, S), BF16),
             pltpu.VMEM((QUAD, K, S), BF16),
             pltpu.VMEM((QUAD, K + 16, S), BF16),
-            pltpu.VMEM((QUAD, K, K), F32),
-            pltpu.VMEM((QUAD, K, K), F32),
+            pltpu.VMEM((QUAD, 2 * K, K), F32),
+            pltpu.VMEM((QUAD, 2 * K, K), BF16),
+            pltpu.VMEM((QUAD, 2 * K, K), BF16),
+            pltpu.VMEM((QUAD, K, K), BF16),
+            pltpu.VMEM((QUAD, K, K), BF16),
+            pltpu.VMEM((QUAD, K, K), BF16),
             pltpu.VMEM((QUAD, 1, S), F32),
+            pltpu.SemaphoreType.DMA((4,)),
             pltpu.SemaphoreType.DMA((GROUPS,)),
             pltpu.SemaphoreType.DMA((GROUPS,)),
             pltpu.SemaphoreType.DMA((GROUPS, 2)),
@@ -296,9 +326,9 @@
             pltpu.SemaphoreType.DMA((GROUPS, 2)),
         ],
         compiler_params=pltpu.CompilerParams(
-            collective_id=0, has_side_effects=True, vmem_limit_bytes=56 * 1024 * 1024
+            collective_id=0, has_side_effects=True, vmem_limit_bytes=24 * 1024 * 1024
         ),
-    )(pairs, obs_site, obs_blocks, obs_precision, obs_innovation)
+    )(*[pltpu.with_memory_space_constraint(arg, pltpu.HBM) for arg in (pairs, obs_site, obs_blocks, obs_precision, obs_innovation)])
     result = result.reshape(2, DEVICES, 4, PATCHES, 128).transpose(0, 1, 3, 2, 4)
     return result.reshape(2, DEVICES * PATCHES, S)
 

time: 71.1 us -> 61.3 us (0.86)
  Pallas kernels: 67.9 us -> 59.9 us
  local copies, waits for them, and re-layouts: 3.05 us -> 1.32 us
    pallas_call x1, Pallas kernels: 67.9 us -> 59.9 us  [local(): pl.pallas_call(kernel, out_shape=jax.ShapeDtypeStruct(pairs.shape, BF16),...]
    unnamed x1, local copies, waits for them, and re-layouts: 3.05 us -> 1.32 us
where the time goes in v1:
time: 61.3 us; the launch traced here: 61.2 us
  Pallas kernels  59.9 us (98%)
  local copies, waits for them, and re-layouts  1.32 us (2%)
    pallas_call x1, Pallas kernels, local(): pl.pallas_call(kernel, out_shape=jax.ShapeDtypeStruct(pairs.shape, BF16),...  59.9 us
    unnamed x1, local copies, waits for them, and re-layouts  1.32 us

profile of v1, /device:TPU:1, one launch (start us, length us, event | category | flops | bytes accessed | tf_op | source)
XLA Modules:
  0.0 61.2 jit_solution(10074773624690974489)
XLA Ops:
  0.0 59.9 %shard_map.55 = bf16[2,128,4,2,4,128]{5,4,3,2,1,0:T(4,128)(2,1)S(1)} custom-call(bf16[2,128,4,2,4,128]{5,4,3,2,1,0:T(4,128)(2,1)} %bitcast.11, s32[8,2048]{1,0:T(8,128)} %site_hbm.1, s32[8]{0:T(128)} %blocks_hbm.1, bf16[8,2048]{1,0:T(8,128)(2,1)} %precision_hbm.1, bf16[8,2048]{1,0:T(8,128)(2,1)} %innovation_hbm.1), custom_call_target="tpu_custom_call" | custom-call | tf_op jit(solution)/shard_map/pallas_call | solution.py:292
  59.9 1.3 %copy.7 = bf16[2,1024,512]{2,1,0:T(8,128)(2,1)} copy(bf16[2,1024,512]{2,1,0:T(8,128)(2,1)S(1)} %bitcast.10) | data formatting | bytes 4194304

commit v2 on v1

--- a/solution.py
+++ b/solution.py
@@ -40,28 +40,28 @@
     return lax.broadcasted_iota(jnp.int32, shape, axis)
 
 
-def peer(member, region, offset):
-    x = lax.rem(lax.rem(region, 4) + lax.rem(offset, 4), 4)
-    y = lax.rem(lax.div(region, 4) + lax.rem(lax.div(offset, 4), 4), 4)
-    z = lax.rem(lax.div(member, 2) + lax.rem(lax.div(offset, 16), 4), 4)
-    core = lax.rem(lax.rem(member, 2) + lax.div(offset, 64), 2)
-    return z * 2 + core, y * 4 + x
-
-
-def enter(member, region):
-    barrier = pltpu.get_barrier_semaphore()
-    members = [lax.rem(member + step, 8) for step in range(8)]
-    regions = [lax.rem(region + step, 16) for step in range(16)]
-    for outer in range(8):
-        for inner in range(16):
-            if outer or inner:
-                pl.semaphore_signal(
-                    barrier,
-                    inc=1,
-                    device_id=(members[outer], regions[inner]),
-                    device_id_type=MESH,
-                )
-    pl.semaphore_wait(barrier, DEVICES - 1)
+def hops(offset):
+    return sum(min(step, 4 - step) for step in (offset % 4, offset // 4 % 4, offset // 16 % 4))
+
+
+def spread(offset):
+    return offset * STRIDE % DEVICES
+
+
+OTHERS = sorted(range(1, DEVICES), key=spread)
+FARTHEST_FIRST = sorted(OTHERS, key=lambda offset: (-hops(offset), spread(offset)))
+
+
+def neighbours(member, region):
+    xs = [lax.rem(lax.rem(region, 4) + step, 4) for step in range(4)]
+    ys = [lax.rem(lax.div(region, 4) + step, 4) * 4 for step in range(4)]
+    zs = [lax.rem(lax.div(member, 2) + step, 4) * 2 for step in range(4)]
+    cores = [lax.rem(lax.rem(member, 2) + step, 2) for step in range(2)]
+
+    def at(offset):
+        return zs[offset // 16 % 4] + cores[offset // 64], ys[offset // 4 % 4] + xs[offset % 4]
+
+    return at
 
 
 def histogram(site_ref, blocks_ref, weight32, value32, weights, sides):
@@ -203,24 +203,28 @@
     )
     for move in moves:
         move.start()
-    enter(member, region)
-
-    for group in range(GROUPS):
-        def send(index, carry):
-            to_member, to_region = peer(member, region, lax.rem(index * STRIDE, DEVICES))
-            to = to_member * 16 + to_region
+    at = neighbours(member, region)
+
+    def send_in(group, offsets):
+        for offset in offsets:
+            device = at(offset)
             for row in range(2):
                 pltpu.make_async_remote_copy(
-                    src_ref=ens_ref.at[row, to, :, group],
+                    src_ref=ens_ref.at[row, device[0] * 16 + device[1], :, group],
                     dst_ref=inbox.at[group, :, me, row],
                     send_sem=in_send.at[group],
                     recv_sem=in_recv.at[group],
-                    device_id=(to_member, to_region),
+                    device_id=device,
                     device_id_type=MESH,
                 ).start()
-            return carry
-
-        lax.fori_loop(1, DEVICES, send, 0)
+
+    barrier = pltpu.get_barrier_semaphore()
+    for offset in FARTHEST_FIRST:
+        pl.semaphore_signal(barrier, inc=1, device_id=at(offset), device_id_type=MESH)
+    pl.semaphore_wait(barrier, DEVICES - 1)
+    send_in(0, OTHERS)
+    send_in(1, OTHERS)
+    for group in range(GROUPS):
         for row in range(2):
             pltpu.make_async_copy(
                 ens_ref.at[row, me, :, group], inbox.at[group, :, me, row], in_own.at[group, row]
@@ -249,21 +253,17 @@
             group, inbox, outbox, place_in, place_out, weights, sides, state, pert, work, iterate, high_part, low_part, product, product_low, coef, mean
         )
 
-        def send(index, carry):
-            to_member, to_region = peer(member, region, lax.rem(index * STRIDE, DEVICES))
-            to = to_member * 16 + to_region
+        for offset in FARTHEST_FIRST:
+            device = at(offset)
             for row in range(2):
                 pltpu.make_async_remote_copy(
-                    src_ref=outbox.at[group, :, to, row],
+                    src_ref=outbox.at[group, :, device[0] * 16 + device[1], row],
                     dst_ref=out_ref.at[row, me, :, group],
                     send_sem=out_send,
                     recv_sem=out_recv,
-                    device_id=(to_member, to_region),
+                    device_id=device,
                     device_id_type=MESH,
                 ).start()
-            return carry
-
-        lax.fori_loop(1, DEVICES, send, 0)
         for row in range(2):
             pltpu.make_async_copy(
                 outbox.at[group, :, me, row], out_ref.at[row, me, :, group], out_own.at[group, row]

time: 61.3 us -> 60.4 us (0.985)
  Pallas kernels: 59.9 us -> 59 us
    pallas_call x1, Pallas kernels: 59.9 us -> 59 us  [local(): pl.pallas_call(kernel, out_shape=jax.ShapeDtypeStruct(pairs.shape, BF16),...]
where the time goes in v2:
time: 60.4 us; the launch traced here: 60.3 us
  Pallas kernels  59 us (98%)
  local copies, waits for them, and re-layouts  1.32 us (2%)
    pallas_call x1, Pallas kernels, local(): pl.pallas_call(kernel, out_shape=jax.ShapeDtypeStruct(pairs.shape, BF16),...  59 us
    unnamed x1, local copies, waits for them, and re-layouts  1.32 us

profile of v2, /device:TPU:1, one launch (start us, length us, event | category | flops | bytes accessed | tf_op | source)
XLA Modules:
  0.0 60.3 jit_solution(11478573722777240101)
XLA Ops:
  0.0 59.0 %shard_map.55 = bf16[2,128,4,2,4,128]{5,4,3,2,1,0:T(4,128)(2,1)S(1)} custom-call(bf16[2,128,4,2,4,128]{5,4,3,2,1,0:T(4,128)(2,1)} %bitcast.11, s32[8,2048]{1,0:T(8,128)} %site_hbm.1, s32[8]{0:T(128)} %blocks_hbm.1, bf16[8,2048]{1,0:T(8,128)(2,1)} %precision_hbm.1, bf16[8,2048]{1,0:T(8,128)(2,1)} %innovation_hbm.1), custom_call_target="tpu_custom_call" | custom-call | tf_op jit(solution)/shard_map/pallas_call | solution.py:292
  59.0 1.3 %copy.7 = bf16[2,1024,512]{2,1,0:T(8,128)(2,1)} copy(bf16[2,1024,512]{2,1,0:T(8,128)(2,1)S(1)} %bitcast.10) | data formatting | bytes 4194304

commit v3 on v2

--- a/solution.py
+++ b/solution.py
@@ -64,7 +64,7 @@
     return at
 
 
-def histogram(site_ref, blocks_ref, weight32, value32, weights, sides):
+def histogram(site_ref, blocks_ref, weight32, value32, tables):
     lanes = iota((1, SLOTS), 1)
     rows = iota((16, SLOTS), 0)
     quarter = lax.rem(rows, 4)
@@ -80,8 +80,7 @@
         upper = jnp.where(quarter == lax.shift_right_logical(site, 7), picked, 0.0).astype(BF16)
         lower = jnp.where(iota((128, SLOTS), 0) == jnp.bitwise_and(site, 127), 1.0, 0.0).astype(BF16)
         sums = dot_t(upper, lower)
-        weights[patch] = sums[0:4]
-        sides[patch] = sums[4:8] + sums[8:12]
+        tables[patch] = sums
         return carry
 
     lax.fori_loop(0, PATCHES, one, 0)
@@ -91,9 +90,9 @@
     return jnp.concatenate([table[part : part + 1, :] for part in range(4)], axis=1)
 
 
-def analyse(group, inbox, outbox, place_in, place_out, weights, sides, state, pert, work, iterate, high_part, low_part, product, product_low, coef, mean):
-    landed = inbox.reshape(GROUPS, 4, 4 * K, 128)
-    leaving = outbox.reshape(GROUPS, 4, 4 * K, 128)
+def analyse(group, inbox, outbox, place_in, place_out, tables, state, pert, work, iterate, high_part, low_part, product, product_low, coef, mean):
+    landed = inbox.reshape(GROUPS + 1, 4, 4 * K, 128)
+    leaving = outbox.reshape(GROUPS + 1, 4, 4 * K, 128)
     quads = range(QUAD)
 
     for block in range(4):
@@ -109,13 +108,14 @@
     eye = jnp.where(iota((K, K), 0) == iota((K, K), 1), 1.0, 0.0).astype(F32)
     scales, rights = [], []
     for quad in quads:
+        table = tables[group * QUAD + quad]
         values = state[quad].astype(F32)
         centre = jnp.sum(values, axis=0, keepdims=True) * (1.0 / K)
-        mean[quad] = centre
+        mean[quad] = jnp.broadcast_to(centre, (8, S))
         around = (values - centre).astype(BF16)
         pert[quad] = around
-        work[quad, 0:K, :] = (around.astype(F32) * as_row(weights[group * QUAD + quad])).astype(BF16)
-        side = as_row(sides[group * QUAD + quad])
+        work[quad, 0:K, :] = (around.astype(F32) * as_row(table[0:4])).astype(BF16)
+        side = as_row(table[4:8] + table[8:12])
         high = side.astype(BF16).astype(F32)
         work[quad, K : K + 16, :] = jnp.where(
             iota((16, S), 0) == 0, high, jnp.where(iota((16, S), 0) == 1, side - high, 0.0)
@@ -174,7 +174,7 @@
         factor = grown * jnp.sqrt(255.0 / scales[quad])
         coef[quad] = (twice * (grown * grown / scales[quad]) + factor * z).astype(BF16)
     for quad in quads:
-        state[quad] = (mean[quad] + dot(coef[quad], pert[quad])).astype(BF16)
+        state[quad] = (mean[quad, 0:1] + dot(coef[quad], pert[quad])).astype(BF16)
 
     for block in range(4):
         rows = slice(256 * block, 256 * block + 256)
@@ -189,7 +189,7 @@
 
 def kernel(
     ens_ref, site_hbm, blocks_hbm, precision_hbm, innovation_hbm, out_ref,
-    site_ref, blocks_ref, precision_ref, innovation_ref, inbox, outbox, place_in, place_out, weight32, value32, weights, sides, state, pert, work, iterate, high_part, low_part, product, product_low, coef, mean,
+    site_ref, blocks_ref, precision_ref, innovation_ref, inbox, outbox, place_in, place_out, weight32, value32, tables, state, pert, work, iterate, high_part, low_part, product, product_low, coef, mean,
     obs_sem, in_send, in_recv, in_own, out_send, out_recv, out_own,
 ):
     member, region = lax.axis_index("member"), lax.axis_index("region")
@@ -239,7 +239,7 @@
         move.wait()
     weight32[...] = precision_ref[...].astype(F32)
     value32[...] = innovation_ref[...].astype(F32)
-    histogram(site_ref, blocks_ref, weight32, value32, weights, sides)
+    histogram(site_ref, blocks_ref, weight32, value32, tables)
 
     def one_group(group, carry):
         for row in range(2):
@@ -250,7 +250,7 @@
         pltpu.make_async_copy(arrived, arrived, in_recv.at[group]).wait()
 
         analyse(
-            group, inbox, outbox, place_in, place_out, weights, sides, state, pert, work, iterate, high_part, low_part, product, product_low, coef, mean
+            group, inbox, outbox, place_in, place_out, tables, state, pert, work, iterate, high_part, low_part, product, product_low, coef, mean
         )
 
         for offset in FARTHEST_FIRST:
@@ -279,7 +279,7 @@
             pltpu.make_async_copy(
                 outbox.at[group, :, me, row], out_ref.at[row, me, :, group], out_own.at[group, row]
             ).wait()
-    sent = outbox.at[:, :, pl.ds(0, DEVICES - 1)]
+    sent = outbox.at[pl.ds(0, GROUPS), :, pl.ds(0, DEVICES - 1)]
     pltpu.make_async_copy(sent, sent, out_send).wait()
     arrived = out_ref.at[:, pl.ds(0, DEVICES - 1)]
     pltpu.make_async_copy(arrived, arrived, out_recv).wait()
@@ -299,14 +299,13 @@
             pltpu.SMEM((PATCHES,), jnp.int32),
             pltpu.VMEM((PATCHES, SLOTS), BF16),
             pltpu.VMEM((PATCHES, SLOTS), BF16),
-            pltpu.VMEM((GROUPS, 4, DEVICES, 2, QUAD, 128), BF16),
-            pltpu.VMEM((GROUPS, 4, DEVICES, 2, QUAD, 128), BF16),
+            pltpu.VMEM((GROUPS + 1, 4, DEVICES, 2, QUAD, 128), BF16),
+            pltpu.VMEM((GROUPS + 1, 4, DEVICES, 2, QUAD, 128), BF16),
             pltpu.VMEM((256, 256), BF16),
             pltpu.VMEM((256, 256), BF16),
             pltpu.VMEM((PATCHES, SLOTS), F32),
             pltpu.VMEM((PATCHES, SLOTS), F32),
-            pltpu.VMEM((PATCHES, 4, 128), F32),
-            pltpu.VMEM((PATCHES, 4, 128), F32),
+            pltpu.VMEM((PATCHES, 16, 128), F32),
             pltpu.VMEM((QUAD, K, S), BF16),
             pltpu.VMEM((QUAD, K, S), BF16),
             pltpu.VMEM((QUAD, K + 16, S), BF16),
@@ -316,7 +315,7 @@
             pltpu.VMEM((QUAD, K, K), BF16),
             pltpu.VMEM((QUAD, K, K), BF16),
             pltpu.VMEM((QUAD, K, K), BF16),
-            pltpu.VMEM((QUAD, 1, S), F32),
+            pltpu.VMEM((QUAD, 8, S), F32),
             pltpu.SemaphoreType.DMA((4,)),
             pltpu.SemaphoreType.DMA((GROUPS,)),
             pltpu.SemaphoreType.DMA((GROUPS,)),

time: 60.4 us -> 60.4 us (level)
  no operation moved by 1% of the time
where the time goes in v3:
time: 60.4 us; the launch traced here: 60.3 us
  Pallas kernels  58.9 us (98%)
  local copies, waits for them, and re-layouts  1.32 us (2%)
    pallas_call x1, Pallas kernels, local(): pl.pallas_call(kernel, out_shape=jax.ShapeDtypeStruct(pairs.shape, BF16),...  58.9 us
    unnamed x1, local copies, waits for them, and re-layouts  1.32 us

profile of v3, /device:TPU:1, one launch (start us, length us, event | category | flops | bytes accessed | tf_op | source)
XLA Modules:
  0.0 60.3 jit_solution(12908883205081403679)
XLA Ops:
  0.0 58.9 %shard_map.55 = bf16[2,128,4,2,4,128]{5,4,3,2,1,0:T(4,128)(2,1)S(1)} custom-call(bf16[2,128,4,2,4,128]{5,4,3,2,1,0:T(4,128)(2,1)} %bitcast.11, s32[8,2048]{1,0:T(8,128)} %site_hbm.1, s32[8]{0:T(128)} %blocks_hbm.1, bf16[8,2048]{1,0:T(8,128)(2,1)} %precision_hbm.1, bf16[8,2048]{1,0:T(8,128)(2,1)} %innovation_hbm.1), custom_call_target="tpu_custom_call" | custom-call | tf_op jit(solution)/shard_map/pallas_call | solution.py:292
  58.9 1.3 %copy.7 = bf16[2,1024,512]{2,1,0:T(8,128)(2,1)} copy(bf16[2,1024,512]{2,1,0:T(8,128)(2,1)S(1)} %bitcast.10) | data formatting | bytes 4194304

commit v4 on v3

--- a/solution.py
+++ b/solution.py
@@ -50,6 +50,9 @@
 
 OTHERS = sorted(range(1, DEVICES), key=spread)
 FARTHEST_FIRST = sorted(OTHERS, key=lambda offset: (-hops(offset), spread(offset)))
+MIXED = [
+    FARTHEST_FIRST[turn // 2 if turn % 2 == 0 else DEVICES - 2 - turn // 2] for turn in range(DEVICES - 1)
+]
 
 
 def neighbours(member, region):
@@ -222,8 +225,8 @@
     for offset in FARTHEST_FIRST:
         pl.semaphore_signal(barrier, inc=1, device_id=at(offset), device_id_type=MESH)
     pl.semaphore_wait(barrier, DEVICES - 1)
-    send_in(0, OTHERS)
-    send_in(1, OTHERS)
+    send_in(0, MIXED)
+    send_in(1, MIXED)
     for group in range(GROUPS):
         for row in range(2):
             pltpu.make_async_copy(

time: 60.4 us -> 60.1 us (level)
  no operation moved by 1% of the time
where the time goes in v4:
time: 60.1 us; the launch traced here: 60 us
  Pallas kernels  58.6 us (98%)
  local copies, waits for them, and re-layouts  1.32 us (2%)
    pallas_call x1, Pallas kernels, local(): pl.pallas_call(kernel, out_shape=jax.ShapeDtypeStruct(pairs.shape, BF16),...  58.6 us
    unnamed x1, local copies, waits for them, and re-layouts  1.32 us

profile of v4, /device:TPU:1, one launch (start us, length us, event | category | flops | bytes accessed | tf_op | source)
XLA Modules:
  0.0 60.0 jit_solution(16809471139710481032)
XLA Ops:
  0.0 58.6 %shard_map.55 = bf16[2,128,4,2,4,128]{5,4,3,2,1,0:T(4,128)(2,1)S(1)} custom-call(bf16[2,128,4,2,4,128]{5,4,3,2,1,0:T(4,128)(2,1)} %bitcast.11, s32[8,2048]{1,0:T(8,128)} %site_hbm.1, s32[8]{0:T(128)} %blocks_hbm.1, bf16[8,2048]{1,0:T(8,128)(2,1)} %precision_hbm.1, bf16[8,2048]{1,0:T(8,128)(2,1)} %innovation_hbm.1), custom_call_target="tpu_custom_call" | custom-call | tf_op jit(solution)/shard_map/pallas_call | solution.py:295
  58.7 1.3 %copy.7 = bf16[2,1024,512]{2,1,0:T(8,128)(2,1)} copy(bf16[2,1024,512]{2,1,0:T(8,128)(2,1)S(1)} %bitcast.10) | data formatting | bytes 4194304
